TPU v7x, 512 devices: a whole 4x4x16 slice. The times are simulated.
512 devices in a mesh: row: 64 (over z_hi, y, x), col: 8 (over z_lo, core).
Axes of the slice: x: 4, y: 4, z: 16 (z_hi: 4, z_lo: 4; z = z_hi * 4 + z_lo), core: 2. Of those that a mesh axis runs over, the one named last changes fastest.
Arguments:
- species: float32 [2, 512, 512, 256], P(None, None, 'row', 'col'), may hold values from -6 to 6
- symbol_x: float32 [512], replicated, may hold values from 0.3 to 3
- symbol_y: float32 [512], replicated, may hold values from 0.3 to 3
- symbol_z: float32 [256], replicated, may hold values from 0.3 to 3
Outputs:
- spectrum: float32 [2, 512, 512, 256], P(None, 'row', 'col')
All inputs are finite; a program needn't handle non-finite values.
Results may differ from a plain program's by a relative error of at most 0.00007.
Values sent between devices are 32-bit elements; how exact they have to be, the bound alone decides.
A program may use at most 64 MiB of HBM per device.

v0:
```python
import jax
import jax.numpy as jnp
from jax import lax
from jax.sharding import PartitionSpec as P


def basis_table(count):
    rank = jnp.arange(count)
    angle = (
        jnp.pi
        / (4 * count)
        * ((2 * rank[:, None] + 1) * (2 * rank[None, :] + 1) % (8 * count)).astype(jnp.float32)
    )
    return jnp.cos(angle) * (2.0 / count) ** 0.5


def to_modes(values, dim):
    moved = jnp.tensordot(
        values, basis_table(values.shape[dim]), axes=([dim], [0]), precision=lax.Precision.HIGHEST
    )
    return jnp.moveaxis(moved, -1, dim)


def on_device(species, symbol_x, symbol_y, symbol_z):
    part_values = species
    part_values = to_modes(part_values, 1)
    part_values = lax.all_to_all(part_values, "row", split_axis=1, concat_axis=2, tiled=True)
    part_values = to_modes(part_values, 2)
    local_values = part_values
    local_values = lax.all_to_all(local_values, "col", split_axis=2, concat_axis=3, tiled=True)
    local_values = to_modes(local_values, 3)
    share_x = local_values.shape[1]
    part_x = lax.dynamic_slice_in_dim(symbol_x, lax.axis_index("row") * share_x, share_x)
    share_y = local_values.shape[2]
    part_y = lax.dynamic_slice_in_dim(symbol_y, lax.axis_index("col") * share_y, share_y)
    symbol = part_x[:, None, None] + part_y[None, :, None] + symbol_z[None, None, :]
    local_values = local_values / symbol
    return local_values


def solution(mesh):
    in_specs = (P(None, None, "row", "col"), P(), P(), P())
    out_specs = P(None, "row", "col", None)
    return jax.shard_map(
        on_device, mesh=mesh, in_specs=in_specs, out_specs=out_specs, check_vma=False
    )
```

profile of v0, /device:TPU:1, one launch (start us, length us, event | category | flops | bytes accessed | tf_op | source)
XLA Modules:
  0.0 166.1 jit_solution(4326028335347048153)
XLA Ops:
  0.0 0.0 copy-start
  0.0 1.2 copy-done
  1.2 5.8 %fusion.13 = f32[512,512]{0,1:S(1)} fusion(f32[512,512]{0,1:T(8,128)S(1)} %bitcast.36, s32[512]{0:T(512)S(1)} %multiply_add_fusion), kind=kOutput, calls=%fused_computation.16 | convolution fusion | flops 1614544896 | bytes 2099200
  7.0 3.7 %copy.12 = f32[2,512,8,32]{3,2,0,1:T(8,128)} copy(f32[2,512,8,32]{1,3,2,0:T(8,128)S(1)} %bitcast.42) | data formatting | bytes 2097152 | tf_op jit(solution)/shard_map/transpose | solution.py:21
  10.7 3.8 %reshape.66 = f32[64,1,4096]{2,1,0:T(1,128)S(1)} reshape(f32[512,2,8,32]{3,2,1,0:T(8,128)} %bitcast.37) | data formatting | bytes 2097152
  14.5 68.2 %all_to_all.36 = f32[64,1,4096]{2,1,0:T(1,128)S(1)} all-to-all(f32[64,1,4096]{2,1,0:T(1,128)S(1)} %reshape.66), channel_id=1, replica_groups=mesh['row'=64,'col'=8] {'row'}, dimensions={0} | all-to-all | bytes 2097152 | tf_op jit(solution)/shard_map/all_to_all | solution.py:27
  82.7 0.5 broadcast.126
  83.2 3.2 %reduce = f32[64,4096]{1,0:T(8,128)S(1)} reduce(f32[64,1,4096]{2,1,0:T(1,128)S(1)} %all_to_all.36, f32[]{:T(128)} %broadcast.126), dimensions={1}, to_apply=%all_to_all.26.reduce_sub_computation | reduce | bytes 2097156 | tf_op jit(solution)/shard_map/all_to_all | solution.py:27
  86.4 2.7 %reshape.67 = f32[512,2,8,32]{3,2,1,0:T(8,128)} reshape(f32[64,4096]{1,0:T(8,128)S(1)} %reduce) | data formatting | bytes 2097152
  89.1 13.1 %fusion.3 = f32[2,8,512,32]{2,3,1,0:T(8,128)S(1)} fusion(f32[2,8,64,8,32]{4,3,0,1,2:T(8,128)} %bitcast.40, s32[512]{0:T(512)S(1)} %multiply_add_fusion), kind=kOutput, calls=%fused_computation.8 | convolution fusion | flops 1614544896 | bytes 2099200 | tf_op jit(solution)/shard_map/dot_general | solution.py:18
  102.2 3.9 %copy.16 = f32[2,8,512,32]{3,1,0,2:T(8,128)} copy(f32[2,8,512,32]{2,3,1,0:T(8,128)S(1)} %fusion.3) | data formatting | bytes 2097152 | tf_op jit(solution)/shard_map/transpose | solution.py:21
  106.1 0.0 copy-start.1
  106.1 4.8 %reshape.68 = f32[8,1,32768]{2,1,0:T(1,128)} reshape(f32[512,2,8,32]{3,2,1,0:T(8,128)} %bitcast.38) | data formatting | bytes 2097152
  110.9 14.1 %all-to-all-start.1 = ((f32[8,1,32768]{2,1,0:T(1,128)}), f32[8,1,32768]{2,1,0:T(1,128)S(1)}, u32[]{:S(2)}, u32[]{:S(2)}) async-start(f32[8,1,32768]{2,1,0:T(1,128)} %reshape.68), calls=%async_computation.1 | async-start | bytes 2097152 | tf_op jit(solution)/shard_map/all_to_all | solution.py:30
  125.0 0.8 dynamic_slice.7
  125.7 0.8 dynamic_slice.6
  126.5 0.1 broadcast_add_fusion.1
  126.6 0.0 copy-done.1
  126.6 0.9 broadcast_add_fusion
  127.5 23.1 %all-to-all-done.1 = f32[8,1,32768]{2,1,0:T(1,128)S(1)} async-done(((f32[8,1,32768]{2,1,0:T(1,128)}), f32[8,1,32768]{2,1,0:T(1,128)S(1)}, u32[]{:S(2)}, u32[]{:S(2)}) %all-to-all-start.1) | async-done | bytes 1048608 | tf_op jit(solution)/shard_map/all_to_all | solution.py:30
  150.6 3.0 %reduce.1 = f32[8,32768]{1,0:T(8,128)S(1)} reduce(f32[8,1,32768]{2,1,0:T(1,128)S(1)} %all-to-all-done.1, f32[]{:T(128)} %broadcast.126), dimensions={1}, to_apply=%all_to_all.30.reduce_sub_computation | reduce | bytes 2097156 | tf_op jit(solution)/shard_map/all_to_all | solution.py:30
  153.6 3.3 %reshape.69 = f32[512,2,8,32]{3,2,1,0:T(8,128)} reshape(f32[8,32768]{1,0:T(8,128)S(1)} %reduce.1) | data formatting | bytes 2097152
  156.9 2.8 %copy.17 = f32[2,8,8,64,32]{3,4,2,1,0:T(8,128)S(1)} copy(f32[2,8,8,64,32]{4,1,0,3,2:T(8,128)} %bitcast.39) | data formatting | bytes 2097152 | tf_op jit(solution)/shard_map/all_to_all | solution.py:30
  159.8 6.3 %convolution_divide_fusion = f32[2,8,64,256]{3,2,1,0:T(8,128)} fusion(f32[2,8,64,256]{2,3,1,0:T(8,128)S(1)} %bitcast.41, f32[8,64,256]{2,1,0:T(8,128)} %broadcast_add_fusion, s32[256]{0:T(256)S(1)} %multiply_add_fusion.1), kind=kOutput, calls=%fused_computation.9 | convolution fusion | flops 806551552 | bytes 2622464 | tf_op jit(solution)/shard_map/dot_general | solution.py:18
  (2 shorter events, 0.0 us)
Async XLA Ops:
  0.0 1.2 copy-start
  106.1 20.5 %copy-start.1 = (f32[256]{0:T(256)S(1)}, f32[256]{0:T(256)}, u32[]{:S(2)}) copy-start(f32[256]{0:T(256)} %param.7) | copy-start | bytes 3076
  110.9 39.7 %all-to-all-start.1 = ((f32[8,1,32768]{2,1,0:T(1,128)}), f32[8,1,32768]{2,1,0:T(1,128)S(1)}, u32[]{:S(2)}, u32[]{:S(2)}) async-start(f32[8,1,32768]{2,1,0:T(1,128)} %reshape.68), calls=%async_computation.1 | async-start | bytes 2097152 | tf_op jit(solution)/shard_map/all_to_all | solution.py:30
where the time goes:
time: 167 us; the launch traced here: 166 us
  blocking collectives  68.2 us (41%)
  local copies, waits for them, and re-layouts  28.3 us (17%)
  matrix products  25.2 us (15%)
  waiting for transfers between devices  23.1 us (14%)
  starting transfers between devices  14.1 us (8%)
  other arithmetic  7.2 us (4%)
    all_to_all x1, blocking collectives, on_device(): lax.all_to_all(part_values, 'row', split_axis=1, concat_axis=2, tiled=True)  68.2 us
    all_to_all x1, waiting for transfers between devices, on_device(): lax.all_to_all(local_values, 'col', split_axis=2, concat_axis=3, tiled=True)  23.1 us
    dot_general x2, matrix products, to_modes(): jnp.tensordot(values, basis_table(values.shape[dim]), axes=([dim], [0]),...  19.4 us
    unnamed x8, local copies, waits for them, and re-layouts  15.9 us
    all_to_all x1, starting transfers between devices, on_device(): lax.all_to_all(local_values, 'col', split_axis=2, concat_axis=3, tiled=True)  14.1 us
    transpose x2, local copies, waits for them, and re-layouts, to_modes(): return jnp.moveaxis(moved, -1, dim)  7.53 us
    unnamed x1, matrix products  5.78 us
  transfers between devices with their start and end apart: 1, of which 1 were waited for; matrix products, arithmetic and copies ran while one was open for 2% of the time, Pallas kernels for 0%

commit v1 on v0

v1 whole, which is shorter than its diff:
```python
import functools

import jax
import jax.numpy as jnp
import ml_dtypes
import numpy as np
from jax import lax
from jax.experimental import pallas as pl
from jax.experimental.pallas import tpu as pltpu
from jax.sharding import PartitionSpec as P

MESH = pl.DeviceIdType.MESH
F32 = jnp.float32
BF16 = jnp.bfloat16


def split_table(count):
    rank = np.arange(count, dtype=np.float64)
    angle = np.pi / (4 * count) * (2 * rank[:, None] + 1) * (2 * rank[None, :] + 1)
    table = (np.cos(angle) * np.sqrt(2.0 / count)).astype(np.float32)
    high = table.astype(ml_dtypes.bfloat16)
    low = (table - high.astype(np.float32)).astype(ml_dtypes.bfloat16)
    return np.stack([high, low])


def halves(values):
    high = values.astype(BF16)
    return high, (values - high.astype(F32)).astype(BF16)


def product(a, b, dims):
    dot = functools.partial(
        lax.dot_general, dimension_numbers=(dims, ((), ())), preferred_element_type=F32
    )
    return dot(a[0], b[0]) + dot(a[0], b[1]) + dot(a[1], b[0])


def swap_granules(v0, v1):
    sub = lax.broadcasted_iota(jnp.int32, (8, 128), 0)
    lane = lax.broadcasted_iota(jnp.int32, (8, 128), 1)
    upper = sub >= 4
    w0 = jnp.where(upper, pltpu.roll(v1, 4, 0), v0)
    w1 = jnp.where(upper, v1, pltpu.roll(v0, 4, 0))
    s1, g1 = (sub // 2) % 2, lane // 64
    s0, g0 = sub % 2, (lane // 32) % 2
    out = []
    for w in (w0, w1):
        u = pltpu.roll(w, 64, 1)
        w = jnp.where(
            s1 == g1, w, jnp.where(s1 == 0, pltpu.roll(u, 6, 0), pltpu.roll(u, 2, 0))
        )
        a, b = pltpu.roll(w, 32, 1), pltpu.roll(w, 96, 1)
        w = jnp.where(
            s0 == g0, w, jnp.where(s0 == 0, pltpu.roll(a, 7, 0), pltpu.roll(b, 1, 0))
        )
        out.append(w)
    return out


def swap_four(v):
    lane = lax.broadcasted_iota(jnp.int32, (8, 128), 1)
    g1, g0 = lane // 64 == 1, (lane // 32) % 2 == 1
    w = [None] * 4
    for k in range(2):
        a, b = v[k], v[k + 2]
        w[k] = jnp.where(g1, pltpu.roll(b, 64, 1), a)
        w[k + 2] = jnp.where(g1, b, pltpu.roll(a, 64, 1))
    o = [None] * 4
    for k in (0, 2):
        a, b = w[k], w[k + 1]
        o[k] = jnp.where(g0, pltpu.roll(b, 32, 1), a)
        o[k + 1] = jnp.where(g0, b, pltpu.roll(a, 96, 1))
    return o


def kernel(
    rows, cols, x_hbm, h_hbm, hz_hbm, sx_hbm, sy_hbm, sz_hbm, out, symbol,
    x, h, hz, sx, sy, sz, mid, to_row, from_row, to_col, from_col, line,
    load_sem, send_sem, recv_sem,
):
    row, col = lax.axis_index("row"), lax.axis_index("col")
    fields = x.shape[0]

    barrier = pltpu.get_barrier_semaphore()

    @pl.loop(1, rows)
    def _(i):
        peer = (lax.rem(row + i, rows), col)
        pl.semaphore_signal(barrier, inc=1, device_id=peer, device_id_type=MESH)

    @pl.loop(1, cols)
    def _(i):
        peer = (row, lax.rem(col + i, cols))
        pl.semaphore_signal(barrier, inc=1, device_id=peer, device_id_type=MESH)

    loads = [
        pltpu.make_async_copy(src, dst, load_sem.at[k])
        for k, (src, dst) in enumerate(
            [
                (h_hbm, h),
                (x_hbm.at[0], x.at[0]),
                (x_hbm.at[1], x.at[1]),
                (hz_hbm, hz),
                (sx_hbm, sx),
                (sy_hbm, sy),
                (sz_hbm, sz),
            ]
        )
    ]
    for load in loads:
        load.start()
    loads[0].wait()

    def first(f):
        loads[1 + f].wait()
        mid[...] = product((h[0], h[1]), halves(x[f]), ((1,), (1,)))

        @pl.loop(0, rows // 4)
        def _(g):
            for k in range(4):
                peer = g * 4 + k
                at = pl.ds(pl.multiple_of(peer * 8, 8), 8)
                v = swap_granules(mid[at, :128], mid[at, 128:])
                to_row[f, peer, :, :128] = v[0]
                to_row[f, peer, :, 128:] = v[1]

        from_row[f, row] = to_row[f, row]

    def row_copy(f, peer):
        return pltpu.make_async_remote_copy(
            to_row.at[f, peer], from_row.at[f, row], send_sem.at[f], recv_sem.at[f],
            device_id=(peer, col), device_id_type=MESH,
        )

    def send_rows(f):
        @pl.loop(1, rows)
        def _(i):
            row_copy(f, lax.rem(row + i, rows)).start()

    def all_rows(f):
        return pltpu.make_async_remote_copy(
            to_row.at[f, pl.ds(0, rows - 1)], from_row.at[f, pl.ds(0, rows - 1)],
            send_sem.at[f], recv_sem.at[f],
            device_id=(lax.rem(row + 1, rows), col), device_id_type=MESH,
        )

    def second(f):
        lines = from_row[f].reshape(rows * 8, 256)
        modes = product((h[0], h[1]), halves(lines), ((1,), (0,)))
        to_col[f] = modes.reshape(cols, 64, 256)
        from_col[f, col] = to_col[f, col]

    def send_cols(f):
        for i in range(1, cols):
            peer = lax.rem(col + i, cols)
            pltpu.make_async_remote_copy(
                to_col.at[f, peer], from_col.at[f, col],
                send_sem.at[2 + f], recv_sem.at[2 + f],
                device_id=(row, peer), device_id_type=MESH,
            ).start()

    def all_cols(f):
        return pltpu.make_async_remote_copy(
            to_col.at[f, pl.ds(0, cols - 1)], from_col.at[f, pl.ds(0, cols - 1)],
            send_sem.at[2 + f], recv_sem.at[2 + f],
            device_id=(row, lax.rem(col + 1, cols)), device_id_type=MESH,
        )

    def third(f):
        @pl.loop(0, 8)
        def _(g):
            at = pl.ds(pl.multiple_of(g * 8, 8), 8)
            for i in range(2):
                for j in range(2):
                    lanes, to = pl.ds(128 * i, 128), pl.ds(128 * j, 128)
                    v = swap_four([from_col[f, 4 * j + c, at, lanes] for c in range(4)])
                    for k in range(4):
                        line[4 * i + k, at, to] = v[k]

        lines = line[...].reshape(512, 256)
        modes = product(halves(lines), (hz[0], hz[1]), ((1,), (0,)))
        out[f] = modes.reshape(8, 64, 256)

    def fill_symbol():
        share_x, share_y = symbol.shape[0], symbol.shape[1]
        lane = lax.broadcasted_iota(jnp.int32, (share_y, sy.shape[1]), 1)
        sub = lax.broadcasted_iota(jnp.int32, (share_y, sy.shape[1]), 0)
        mine = lane == col * share_y + sub
        part_y = jnp.sum(jnp.where(mine, sy[...], 0.0), axis=1, keepdims=True)
        lane_x = lax.broadcasted_iota(jnp.int32, sx.shape, 1)
        for k in range(share_x):
            mine = lane_x == row * share_x + k
            part_x = jnp.sum(jnp.where(mine, sx[...], 0.0), axis=1, keepdims=True)
            symbol[k] = (part_x + part_y) + sz[...]

    first(0)
    pl.semaphore_wait(barrier, rows + cols - 2)
    for f in range(fields):
        if f > 0:
            first(f)
        send_rows(f)
    for load in loads[3:]:
        load.wait()
    fill_symbol()
    for f in range(fields):
        all_rows(f).wait_recv()
        second(f)
        send_cols(f)
    for f in range(fields):
        all_cols(f).wait_recv()
        third(f)
    for f in range(fields):
        all_rows(f).wait_send()
        all_cols(f).wait_send()


def on_device(rows, cols, species, symbol_x, symbol_y, symbol_z):
    fields, nx, ny, nz = species.shape
    values = species.transpose(0, 2, 3, 1).reshape(fields, ny * nz, nx)
    table, table_z = jnp.asarray(split_table(nx)), jnp.asarray(split_table(nz * cols))
    share_x, share_y = nx // rows, ny * rows // cols
    anywhere = pl.BlockSpec(memory_space=pl.ANY)
    spectrum, symbol = pl.pallas_call(
        functools.partial(kernel, rows, cols),
        out_shape=[
            jax.ShapeDtypeStruct((fields, share_x, share_y, nz * cols), F32),
            jax.ShapeDtypeStruct((share_x, share_y, nz * cols), F32),
        ],
        in_specs=[anywhere] * 6,
        out_specs=[pl.BlockSpec(memory_space=pltpu.VMEM)] * 2,
        scratch_shapes=[
            pltpu.VMEM(values.shape, F32),
            pltpu.VMEM(table.shape, BF16),
            pltpu.VMEM(table_z.shape, BF16),
            pltpu.VMEM((1, nx), F32),
            pltpu.VMEM((1, ny * rows), F32),
            pltpu.VMEM((1, nz * cols), F32),
            pltpu.VMEM((nx, ny * nz), F32),
            pltpu.VMEM((fields, rows, 8, 256), F32),
            pltpu.VMEM((fields, rows, 8, 256), F32),
            pltpu.VMEM((fields, cols, 64, 256), F32),
            pltpu.VMEM((fields, cols, 64, 256), F32),
            pltpu.VMEM((8, 64, 256), F32),
            pltpu.SemaphoreType.DMA((7,)),
            pltpu.SemaphoreType.DMA((4,)),
            pltpu.SemaphoreType.DMA((4,)),
        ],
        compiler_params=pltpu.CompilerParams(
            collective_id=0, has_side_effects=True, vmem_limit_bytes=60 * 2**20
        ),
    )(values, table, table_z, symbol_x[None], symbol_y[None], symbol_z[None])
    return spectrum / symbol


def solution(mesh):
    in_specs = (P(None, None, "row", "col"), P(), P(), P())
    out_specs = P(None, "row", "col", None)
    return jax.shard_map(
        functools.partial(on_device, mesh.shape["row"], mesh.shape["col"]),
        mesh=mesh, in_specs=in_specs, out_specs=out_specs, check_vma=False,
    )
```

time: 167 us -> 94.1 us (0.56)
  Pallas kernels: 0 us -> 91.2 us
  blocking collectives: 68.2 us -> 0 us
  local copies, waits for them, and re-layouts: 28.3 us -> 0 us
  matrix products: 25.2 us -> 0 us
  waiting for transfers between devices: 23.1 us -> 0 us
  starting transfers between devices: 14.1 us -> 0 us
  other arithmetic: 7.2 us -> 2.45 us
    pallas_call x0 -> x1, Pallas kernels: none -> 91.2 us  [on_device(): pl.pallas_call(functools.partial(kernel, rows, cols), out_shape=[jax.Shap...]
    all_to_all x1 -> x0, blocking collectives: 68.2 us -> none  [on_device(): lax.all_to_all(part_values, 'row', split_axis=1, concat_axis=2, tiled=True)]
    all_to_all x1 -> x0, waiting for transfers between devices: 23.1 us -> none  [on_device(): lax.all_to_all(local_values, 'col', split_axis=2, concat_axis=3, tiled=True)]
    dot_general x2 -> x0, matrix products: 19.4 us -> none  [to_modes(): jnp.tensordot(values, basis_table(values.shape[dim]), axes=([dim], [0]),...]
    unnamed x8 -> x0, local copies, waits for them, and re-layouts: 15.9 us -> none
    all_to_all x1 -> x0, starting transfers between devices: 14.1 us -> none  [on_device(): lax.all_to_all(local_values, 'col', split_axis=2, concat_axis=3, tiled=True)]
    transpose x2 -> x0, local copies, waits for them, and re-layouts: 7.53 us -> none  [to_modes(): return jnp.moveaxis(moved, -1, dim)]
    all_to_all x2 -> x0, other arithmetic: 6.19 us -> none  [the longest x1 3.16 us: on_device(): lax.all_to_all(part_values, 'row', split_axis=1, concat_axis=2, tiled=True)]
  transfers between devices with their start and end apart: 1 -> 0, of which waited for: 1 -> 0; matrix products, arithmetic and copies ran while one was open for 2% -> 0% of each run, Pallas kernels for 0% -> 0%
where the time goes in v1:
time: 94.1 us; the launch traced here: 93.7 us
  Pallas kernels  91.2 us (97%)
  other arithmetic  2.45 us (3%)
    pallas_call x1, Pallas kernels, on_device(): pl.pallas_call(functools.partial(kernel, rows, cols), out_shape=[jax.Shap...  91.2 us
    div x1, other arithmetic, on_device(): return spectrum / symbol  2.45 us

profile of v1, /device:TPU:1, one launch (start us, length us, event | category | flops | bytes accessed | tf_op | source)
XLA Modules:
  0.0 93.7 jit_solution(12840649348406799974)
XLA Ops:
  0.0 91.2 %shard_map.64 = (f32[2,8,64,256]{3,2,1,0:T(8,128)}, f32[8,64,256]{2,1,0:T(8,128)}) custom-call(f32[2,256,512]{2,1,0:T(8,128)} %bitcast.6, bf16[2,512,512]{2,1,0:T(8,128)(2,1)} %constant.4.clone.h_hbm, bf16[2,256,256]{2,1,0:T(8,128)(2,1)} %constant.5.clone.hz_hbm, f32[1,512]{1,0:T(1,128)} %bitcast.7, f32[1,512]{1,0:T(1,128)} %bitcast.8, f32[1,256]{1,0:T(1,128)} %bitcast.9), custom_call_target="tpu_custom_call" | custom-call | tf_op jit(solution)/shard_map/pallas_call | solution.py:223
  91.2 2.5 %broadcast_divide_fusion = f32[2,8,64,256]{3,2,1,0:T(8,128)} fusion(f32[2,8,64,256]{3,2,1,0:T(8,128)} %get-tuple-element.7, f32[8,64,256]{2,1,0:T(8,128)} %get-tuple-element.8), kind=kLoop, calls=%fused_computation | loop fusion | flops 262144 | bytes 2621440 | tf_op jit(solution)/shard_map/div | solution.py:252

commit v2 on v1

--- a/solution.py
+++ b/solution.py
@@ -12,6 +12,7 @@
 MESH = pl.DeviceIdType.MESH
 F32 = jnp.float32
 BF16 = jnp.bfloat16
+GROUPS = 4
 
 
 def split_table(count):
@@ -75,23 +76,30 @@
 
 def kernel(
     rows, cols, x_hbm, h_hbm, hz_hbm, sx_hbm, sy_hbm, sz_hbm, out, symbol,
-    x, h, hz, sx, sy, sz, mid, to_row, from_row, to_col, from_col, line,
-    load_sem, send_sem, recv_sem,
+    x, h, hz, sx, sy, sz, mid, to_row, via, from_row, to_col, from_col, line,
+    load_sem, send_sem, recv_sem, z_send_sem, z_recv_sem, ready_sem,
 ):
     row, col = lax.axis_index("row"), lax.axis_index("col")
-    fields = x.shape[0]
+    plane = rows // GROUPS
+    group, place = row // plane, lax.rem(row, plane)
+
+    def in_group(step):
+        return lax.rem(group + step, GROUPS) * plane
+
+    def signal(semaphore, peer):
+        pl.semaphore_signal(semaphore, inc=1, device_id=peer, device_id_type=MESH)
 
     barrier = pltpu.get_barrier_semaphore()
-
-    @pl.loop(1, rows)
+    for step in (1, GROUPS - 1):
+        signal(barrier, (in_group(step) + place, col))
+
+    @pl.loop(1, plane)
     def _(i):
-        peer = (lax.rem(row + i, rows), col)
-        pl.semaphore_signal(barrier, inc=1, device_id=peer, device_id_type=MESH)
+        signal(barrier, (in_group(0) + lax.rem(place + i, plane), col))
 
     @pl.loop(1, cols)
     def _(i):
-        peer = (row, lax.rem(col + i, cols))
-        pl.semaphore_signal(barrier, inc=1, device_id=peer, device_id_type=MESH)
+        signal(barrier, (row, lax.rem(col + i, cols)))
 
     loads = [
         pltpu.make_async_copy(src, dst, load_sem.at[k])
@@ -124,24 +132,36 @@
                 to_row[f, peer, :, :128] = v[0]
                 to_row[f, peer, :, 128:] = v[1]
 
-        from_row[f, row] = to_row[f, row]
-
-    def row_copy(f, peer):
+    def z_copy(f, step):
+        k = f * 3 + step - 1
         return pltpu.make_async_remote_copy(
-            to_row.at[f, peer], from_row.at[f, row], send_sem.at[f], recv_sem.at[f],
-            device_id=(peer, col), device_id_type=MESH,
-        )
-
-    def send_rows(f):
-        @pl.loop(1, rows)
+            to_row.at[f, pl.ds(in_group(step), plane)], via.at[f, step - 1],
+            z_send_sem.at[k], z_recv_sem.at[k],
+            device_id=(in_group(step) + place, col), device_id_type=MESH,
+        )
+
+    def send_plane(f, step):
+        source = in_group(GROUPS - step) + place if step else row
+
+        def block(q):
+            return via.at[f, step - 1, q] if step else to_row.at[f, row - place + q]
+
+        @pl.loop(1, plane)
         def _(i):
-            row_copy(f, lax.rem(row + i, rows)).start()
+            q = lax.rem(place + i, plane)
+            pltpu.make_async_remote_copy(
+                block(q), from_row.at[f, source], send_sem.at[f], recv_sem.at[f],
+                device_id=(in_group(0) + q, col), device_id_type=MESH,
+            ).start()
+
+        from_row[f, source] = block(place)[...]
 
     def all_rows(f):
+        count = GROUPS * (plane - 1)
         return pltpu.make_async_remote_copy(
-            to_row.at[f, pl.ds(0, rows - 1)], from_row.at[f, pl.ds(0, rows - 1)],
+            to_row.at[f, pl.ds(0, count)], from_row.at[f, pl.ds(0, count)],
             send_sem.at[f], recv_sem.at[f],
-            device_id=(lax.rem(row + 1, rows), col), device_id_type=MESH,
+            device_id=(in_group(1) + place, col), device_id_type=MESH,
         )
 
     def second(f):
@@ -193,23 +213,36 @@
             part_x = jnp.sum(jnp.where(mine, sx[...], 0.0), axis=1, keepdims=True)
             symbol[k] = (part_x + part_y) + sz[...]
 
+    near = (1, GROUPS - 1)
     first(0)
-    pl.semaphore_wait(barrier, rows + cols - 2)
-    for f in range(fields):
-        if f > 0:
-            first(f)
-        send_rows(f)
+    pl.semaphore_wait(barrier, plane + cols)
+    for step in near:
+        z_copy(0, step).start()
+    for step in near:
+        signal(ready_sem, (in_group(step) + place, col))
+    send_plane(0, 0)
+    first(1)
+    pl.semaphore_wait(ready_sem, 2)
+    z_copy(0, 2).start()
+    for step in (*near, 2):
+        z_copy(1, step).start()
+    send_plane(1, 0)
     for load in loads[3:]:
         load.wait()
     fill_symbol()
-    for f in range(fields):
+    for f in range(2):
+        for step in (*near, 2):
+            z_copy(f, step).wait_recv()
+            send_plane(f, step)
         all_rows(f).wait_recv()
         second(f)
         send_cols(f)
-    for f in range(fields):
+    for f in range(2):
         all_cols(f).wait_recv()
         third(f)
-    for f in range(fields):
+    for f in range(2):
+        for step in (*near, 2):
+            z_copy(f, step).wait_send()
         all_rows(f).wait_send()
         all_cols(f).wait_send()
 
@@ -237,6 +270,7 @@
             pltpu.VMEM((1, nz * cols), F32),
             pltpu.VMEM((nx, ny * nz), F32),
             pltpu.VMEM((fields, rows, 8, 256), F32),
+            pltpu.VMEM((fields, GROUPS - 1, rows // GROUPS, 8, 256), F32),
             pltpu.VMEM((fields, rows, 8, 256), F32),
             pltpu.VMEM((fields, cols, 64, 256), F32),
             pltpu.VMEM((fields, cols, 64, 256), F32),
@@ -244,6 +278,9 @@
             pltpu.SemaphoreType.DMA((7,)),
             pltpu.SemaphoreType.DMA((4,)),
             pltpu.SemaphoreType.DMA((4,)),
+            pltpu.SemaphoreType.DMA((6,)),
+            pltpu.SemaphoreType.DMA((6,)),
+            pltpu.SemaphoreType.REGULAR,
         ],
         compiler_params=pltpu.CompilerParams(
             collective_id=0, has_side_effects=True, vmem_limit_bytes=60 * 2**20

time: 94.1 us -> 87.8 us (0.933)
  Pallas kernels: 91.2 us -> 85.1 us
    pallas_call x1, Pallas kernels: 91.2 us -> 85.1 us  [on_device(): pl.pallas_call(functools.partial(kernel, rows, cols), out_shape=[jax.Shap...]
where the time goes in v2:
time: 87.8 us; the launch traced here: 87.6 us
  Pallas kernels  85.1 us (97%)
  other arithmetic  2.45 us (3%)
    pallas_call x1, Pallas kernels, on_device(): pl.pallas_call(functools.partial(kernel, rows, cols), out_shape=[jax.Shap...  85.1 us
    div x1, other arithmetic, on_device(): return spectrum / symbol  2.45 us

profile of v2, /device:TPU:1, one launch (start us, length us, event | category | flops | bytes accessed | tf_op | source)
XLA Modules:
  0.0 87.6 jit_solution(7184462493102852435)
XLA Ops:
  0.0 85.1 %shard_map.64 = (f32[2,8,64,256]{3,2,1,0:T(8,128)}, f32[8,64,256]{2,1,0:T(8,128)}) custom-call(f32[2,256,512]{2,1,0:T(8,128)} %bitcast.6, bf16[2,512,512]{2,1,0:T(8,128)(2,1)} %constant.4.clone.h_hbm, bf16[2,256,256]{2,1,0:T(8,128)(2,1)} %constant.5.clone.hz_hbm, f32[1,512]{1,0:T(1,128)} %bitcast.7, f32[1,512]{1,0:T(1,128)} %bitcast.8, f32[1,256]{1,0:T(1,128)} %bitcast.9), custom_call_target="tpu_custom_call" | custom-call | tf_op jit(solution)/shard_map/pallas_call | solution.py:256
  85.2 2.5 %broadcast_divide_fusion = f32[2,8,64,256]{3,2,1,0:T(8,128)} fusion(f32[2,8,64,256]{3,2,1,0:T(8,128)} %get-tuple-element.7, f32[8,64,256]{2,1,0:T(8,128)} %get-tuple-element.8), kind=kLoop, calls=%fused_computation | loop fusion | flops 262144 | bytes 2621440 | tf_op jit(solution)/shard_map/div | solution.py:289

commit v3 on v2

v3 whole, which is shorter than its diff:
```python
import functools

import jax
import jax.numpy as jnp
import ml_dtypes
import numpy as np
from jax import lax
from jax.experimental import pallas as pl
from jax.experimental.pallas import tpu as pltpu
from jax.sharding import PartitionSpec as P

MESH = pl.DeviceIdType.MESH
F32 = jnp.float32
BF16 = jnp.bfloat16
GROUPS = 4
VMEM_LIMIT = 53500 * 2**10


def split_table(count):
    rank = np.arange(count, dtype=np.float64)
    angle = np.pi / (4 * count) * (2 * rank[:, None] + 1) * (2 * rank[None, :] + 1)
    table = (np.cos(angle) * np.sqrt(2.0 / count)).astype(np.float32)
    high = table.astype(ml_dtypes.bfloat16)
    low = (table - high.astype(np.float32)).astype(ml_dtypes.bfloat16)
    return np.stack([high, low])


def halves(values):
    high = values.astype(BF16)
    return high, (values - high.astype(F32)).astype(BF16)


def product(a, b, dims):
    dot = functools.partial(
        lax.dot_general, dimension_numbers=(dims, ((), ())), preferred_element_type=F32
    )
    return dot(a[0], b[0]) + dot(a[0], b[1]) + dot(a[1], b[0])


def swap_granules(v0, v1):
    sub = lax.broadcasted_iota(jnp.int32, (8, 128), 0)
    lane = lax.broadcasted_iota(jnp.int32, (8, 128), 1)
    upper = sub >= 4
    w0 = jnp.where(upper, pltpu.roll(v1, 4, 0), v0)
    w1 = jnp.where(upper, v1, pltpu.roll(v0, 4, 0))
    s1, g1 = (sub // 2) % 2, lane // 64
    s0, g0 = sub % 2, (lane // 32) % 2
    out = []
    for w in (w0, w1):
        u = pltpu.roll(w, 64, 1)
        w = jnp.where(
            s1 == g1, w, jnp.where(s1 == 0, pltpu.roll(u, 6, 0), pltpu.roll(u, 2, 0))
        )
        a, b = pltpu.roll(w, 32, 1), pltpu.roll(w, 96, 1)
        w = jnp.where(
            s0 == g0, w, jnp.where(s0 == 0, pltpu.roll(a, 7, 0), pltpu.roll(b, 1, 0))
        )
        out.append(w)
    return out


def swap_four(v):
    lane = lax.broadcasted_iota(jnp.int32, (8, 128), 1)
    g1, g0 = lane // 64 == 1, (lane // 32) % 2 == 1
    w = [None] * 4
    for k in range(2):
        a, b = v[k], v[k + 2]
        w[k] = jnp.where(g1, pltpu.roll(b, 64, 1), a)
        w[k + 2] = jnp.where(g1, b, pltpu.roll(a, 64, 1))
    o = [None] * 4
    for k in (0, 2):
        a, b = w[k], w[k + 1]
        o[k] = jnp.where(g0, pltpu.roll(b, 32, 1), a)
        o[k + 1] = jnp.where(g0, b, pltpu.roll(a, 96, 1))
    return o


def kernel(
    rows, cols, x_hbm, h_hbm, out, x, xs, h, hz, mid, to_row, via, from_row, to_col, from_col, line,
    load_sem, send_sem, recv_sem, z_send_sem, z_recv_sem, ready_sem,
):
    row, col = lax.axis_index("row"), lax.axis_index("col")
    plane = rows // GROUPS
    group, place = row // plane, lax.rem(row, plane)

    def in_group(step):
        return lax.rem(group + step, GROUPS) * plane

    def signal(semaphore, peer):
        pl.semaphore_signal(semaphore, inc=1, device_id=peer, device_id_type=MESH)

    barrier = pltpu.get_barrier_semaphore()
    for step in (1, GROUPS - 1):
        signal(barrier, (in_group(step) + place, col))

    @pl.loop(1, plane)
    def _(i):
        signal(barrier, (in_group(0) + lax.rem(place + i, plane), col))

    @pl.loop(1, cols)
    def _(i):
        signal(barrier, (row, lax.rem(col + i, cols)))

    def table_part(step):
        at = pl.ds(pl.multiple_of(in_group(step) * 8, 128), plane * 8)
        return h_hbm.at[:, at, :], h.at[:, at, :]

    near = (1, GROUPS - 1)
    sources = [
        (x_hbm.at[0], x.at[0]),
        table_part(1),
        table_part(GROUPS - 1),
        table_part(2),
        table_part(0),
        (x_hbm.at[1], x.at[1]),
        (h_hbm.at[:, pl.ds(x.shape[2], hz.shape[1]), pl.ds(0, hz.shape[1])], hz),
    ]
    loads = [
        pltpu.make_async_copy(src, dst, load_sem.at[k])
        for k, (src, dst) in enumerate(sources)
    ]
    for load in loads:
        load.start()

    def first(f, step):
        top = pl.multiple_of(in_group(step) * 8, 128)
        at = pl.ds(top, plane * 8)
        mid[...] = product((h[0, at], h[1, at]), (xs[f, 0], xs[f, 1]), ((1,), (1,)))

        @pl.loop(0, plane // 4)
        def _(g):
            for k in range(4):
                here = pl.ds(pl.multiple_of((g * 4 + k) * 8, 8), 8)
                v = swap_granules(mid[here, :128], mid[here, 128:])
                to_row[f, in_group(step) + g * 4 + k, :, :128] = v[0]
                to_row[f, in_group(step) + g * 4 + k, :, 128:] = v[1]

    def split(f):
        xs[f, 0], xs[f, 1] = halves(x[f])

    def z_copy(f, step):
        k = f * 3 + step - 1
        return pltpu.make_async_remote_copy(
            to_row.at[f, pl.ds(in_group(step), plane)], via.at[f, step - 1],
            z_send_sem.at[k], z_recv_sem.at[k],
            device_id=(in_group(step) + place, col), device_id_type=MESH,
        )

    def send_plane(f, step):
        source = in_group(GROUPS - step) + place if step else row

        def block(q):
            return via.at[f, step - 1, q] if step else to_row.at[f, row - place + q]

        @pl.loop(1, plane)
        def _(i):
            q = lax.rem(place + i, plane)
            pltpu.make_async_remote_copy(
                block(q), from_row.at[f, source], send_sem.at[f], recv_sem.at[f],
                device_id=(in_group(0) + q, col), device_id_type=MESH,
            ).start()

        from_row[f, source] = block(place)[...]

    def all_rows(f):
        count = GROUPS * (plane - 1)
        return pltpu.make_async_remote_copy(
            to_row.at[f, pl.ds(0, count)], from_row.at[f, pl.ds(0, count)],
            send_sem.at[f], recv_sem.at[f],
            device_id=(in_group(1) + place, col), device_id_type=MESH,
        )

    def second(f):
        lines = from_row[f].reshape(rows * 8, 256)
        modes = product((h[0], h[1]), halves(lines), ((1,), (0,)))
        for part in range(2):
            lanes = slice(128 * part, 128 * part + 128)
            to_col[f, part] = modes[:, lanes].reshape(cols, 64, 128)
            from_col[f, part, col] = to_col[f, part, col]

    def send_cols(f, part):
        for i in range(1, cols):
            peer = lax.rem(col + i, cols)
            pltpu.make_async_remote_copy(
                to_col.at[f, part, peer], from_col.at[f, part, col],
                send_sem.at[2 + 2 * f + part], recv_sem.at[2 + 2 * f + part],
                device_id=(row, peer), device_id_type=MESH,
            ).start()

    def all_cols(f, part):
        return pltpu.make_async_remote_copy(
            to_col.at[f, part, pl.ds(0, cols - 1)],
            from_col.at[f, part, pl.ds(0, cols - 1)],
            send_sem.at[2 + 2 * f + part], recv_sem.at[2 + 2 * f + part],
            device_id=(row, lax.rem(col + 1, cols)), device_id_type=MESH,
        )

    def third(f, part):
        @pl.loop(0, 8)
        def _(g):
            at = pl.ds(pl.multiple_of(g * 8, 8), 8)
            for j in range(2):
                v = swap_four([from_col[f, part, 4 * j + c, at] for c in range(4)])
                for k in range(4):
                    line[k, at, pl.ds(128 * j, 128)] = v[k]

        lines = line[...].reshape(256, 256)
        modes = product(halves(lines), (hz[0], hz[1]), ((1,), (0,)))
        out[f, 4 * part : 4 * part + 4] = modes.reshape(4, 64, 256)

    loads[0].wait()
    split(0)
    for k, step in enumerate((*near, 2, 0)):
        loads[1 + k].wait()
        first(0, step)
        if k == 0:
            pl.semaphore_wait(barrier, plane + cols)
            for other in near:
                signal(ready_sem, (in_group(other) + place, col))
        if step in near:
            z_copy(0, step).start()
    send_plane(0, 0)
    pl.semaphore_wait(ready_sem, 2)
    z_copy(0, 2).start()
    loads[5].wait()
    split(1)
    for step in (*near, 2, 0):
        first(1, step)
        if step:
            z_copy(1, step).start()
    send_plane(1, 0)
    loads[6].wait()
    for f in range(2):
        for step in (*near, 2):
            z_copy(f, step).wait_recv()
            send_plane(f, step)
        all_rows(f).wait_recv()
        second(f)
        for part in range(2):
            send_cols(f, part)
    for f in range(2):
        for part in range(2):
            all_cols(f, part).wait_recv()
            third(f, part)
    for f in range(2):
        for step in (*near, 2):
            z_copy(f, step).wait_send()
        all_rows(f).wait_send()
        for part in range(2):
            all_cols(f, part).wait_send()


def divide(spectrum, sx, sy, sz, out, done, sems):
    row, col = lax.axis_index("row"), lax.axis_index("col")
    fields, share_x, share_y, nz = spectrum.shape
    lane = lax.broadcasted_iota(jnp.int32, (share_y, sy.shape[1]), 1)
    sub = lax.broadcasted_iota(jnp.int32, (share_y, sy.shape[1]), 0)
    mine = lane == col * share_y + sub
    part_y = jnp.sum(jnp.where(mine, sy[...], 0.0), axis=1, keepdims=True)
    lane_x = lax.broadcasted_iota(jnp.int32, sx.shape, 1)
    copies = []
    for k in range(share_x):
        mine = lane_x == row * share_x + k
        part_x = jnp.sum(jnp.where(mine, sx[...], 0.0), axis=1, keepdims=True)
        symbol = (part_x + part_y) + sz[...]
        for f in range(fields):
            done[f, k] = spectrum[f, k] / symbol
        if k % 2 == 1:
            two = pl.ds(k - 1, 2)
            copies.append(
                pltpu.make_async_copy(done.at[:, two], out.at[:, two], sems.at[k // 2])
            )
            copies[-1].start()
    for copy in copies:
        copy.wait()


def on_device(rows, cols, species, symbol_x, symbol_y, symbol_z):
    fields, nx, ny, nz = species.shape
    values = species.transpose(0, 2, 3, 1).reshape(fields, ny * nz, nx)
    table_z = np.pad(split_table(nz * cols), ((0, 0), (0, 0), (0, nx - nz * cols)))
    table = jnp.asarray(np.concatenate([split_table(nx), table_z], axis=1))
    share_x, share_y = nx // rows, ny * rows // cols
    in_hbm = pl.BlockSpec(memory_space=pltpu.HBM)
    in_vmem = pl.BlockSpec(memory_space=pltpu.VMEM)
    result = jax.ShapeDtypeStruct((fields, share_x, share_y, nz * cols), F32)
    spectrum = pl.pallas_call(
        functools.partial(kernel, rows, cols),
        out_shape=result,
        in_specs=[in_hbm] * 2,
        out_specs=in_vmem,
        scratch_shapes=[
            pltpu.VMEM(values.shape, F32),
            pltpu.VMEM((fields, 2, ny * nz, nx), BF16),
            pltpu.VMEM((2, nx, nx), BF16),
            pltpu.VMEM((2, nz * cols, nz * cols), BF16),
            pltpu.VMEM((nx // GROUPS, ny * nz), F32),
            pltpu.VMEM((fields, rows, 8, 256), F32),
            pltpu.VMEM((fields, GROUPS - 1, rows // GROUPS, 8, 256), F32),
            pltpu.VMEM((fields, rows, 8, 256), F32),
            pltpu.VMEM((fields, 2, cols, 64, 128), F32),
            pltpu.VMEM((fields, 2, cols, 64, 128), F32),
            pltpu.VMEM((4, 64, 256), F32),
            pltpu.SemaphoreType.DMA((7,)),
            pltpu.SemaphoreType.DMA((6,)),
            pltpu.SemaphoreType.DMA((6,)),
            pltpu.SemaphoreType.DMA((6,)),
            pltpu.SemaphoreType.DMA((6,)),
            pltpu.SemaphoreType.REGULAR,
        ],
        compiler_params=pltpu.CompilerParams(
            collective_id=0, has_side_effects=True, vmem_limit_bytes=VMEM_LIMIT
        ),
    )(values, table)
    return pl.pallas_call(
        divide,
        out_shape=result,
        in_specs=[in_vmem] * 4,
        out_specs=in_hbm,
        scratch_shapes=[
            pltpu.VMEM(result.shape, F32),
            pltpu.SemaphoreType.DMA((share_x // 2,)),
        ],
        compiler_params=pltpu.CompilerParams(vmem_limit_bytes=8 * 2**20),
    )(spectrum, symbol_x[None], symbol_y[None], symbol_z[None])


def solution(mesh):
    in_specs = (P(None, None, "row", "col"), P(), P(), P())
    out_specs = P(None, "row", "col", None)
    return jax.shard_map(
        functools.partial(on_device, mesh.shape["row"], mesh.shape["col"]),
        mesh=mesh, in_specs=in_specs, out_specs=out_specs, check_vma=False,
    )
```

time: 87.8 us -> 86.1 us (0.981)
  other arithmetic: 2.45 us -> 0 us
    div x1 -> x0, other arithmetic: 2.45 us -> none  [on_device(): return spectrum / symbol]
    pallas_call x1 -> x2, Pallas kernels: 85.1 us -> 85.9 us  [the longest x1 84.8 us: on_device(): pl.pallas_call(functools.partial(kernel, rows, cols), out_shape=result, i...]
where the time goes in v3:
time: 86.1 us; the launch traced here: 85.9 us
  Pallas kernels  85.9 us (100%)
    pallas_call x1, Pallas kernels, on_device(): pl.pallas_call(functools.partial(kernel, rows, cols), out_shape=result, i...  84.8 us

profile of v3, /device:TPU:1, one launch (start us, length us, event | category | flops | bytes accessed | tf_op | source)
XLA Modules:
  0.0 85.9 jit_solution(9411408084897969507)
XLA Ops:
  0.0 0.0 copy-start
  0.0 0.0 copy-start.1
  0.0 0.0 copy-start.2
  0.0 84.8 %shard_map.55.spectrum = f32[2,8,64,256]{3,2,1,0:T(8,128)S(1)} custom-call(f32[2,256,512]{2,1,0:T(8,128)} %bitcast.9, bf16[2,768,512]{2,1,0:T(8,128)(2,1)} %constant.2.clone.h_hbm), custom_call_target="tpu_custom_call" | custom-call | tf_op jit(solution)/shard_map/pallas_call | solution.py:287
  84.8 0.0 copy-done
  84.8 0.0 copy-done.1
  84.8 0.0 copy-done.2
  84.8 1.1 %shard_map.56 = f32[2,8,64,256]{3,2,1,0:T(8,128)} custom-call(f32[2,8,64,256]{3,2,1,0:T(8,128)S(1)} %shard_map.55.spectrum, f32[1,512]{1,0:T(1,128)S(1)} %bitcast.6, f32[1,512]{1,0:T(1,128)S(1)} %bitcast.7, f32[1,256]{1,0:T(1,128)S(1)} %bitcast.8), custom_call_target="tpu_custom_call" | custom-call | tf_op jit(solution)/shard_map/pallas_call | solution.py:315
Async XLA Ops:
  0.0 84.8 %copy-start = (f32[512]{0:T(512)S(1)}, f32[512]{0:T(512)}, u32[]{:S(2)}) copy-start(f32[512]{0:T(512)} %param.6) | copy-start | bytes 6148
  0.0 84.8 %copy-start.1 = (f32[512]{0:T(512)S(1)}, f32[512]{0:T(512)}, u32[]{:S(2)}) copy-start(f32[512]{0:T(512)} %param.7) | copy-start | bytes 6148
  0.0 84.8 %copy-start.2 = (f32[256]{0:T(256)S(1)}, f32[256]{0:T(256)}, u32[]{:S(2)}) copy-start(f32[256]{0:T(256)} %param.8) | copy-start | bytes 3076

commit v4 on v3

--- a/solution.py
+++ b/solution.py
@@ -77,7 +77,7 @@
 
 def kernel(
     rows, cols, x_hbm, h_hbm, out, x, xs, h, hz, mid, to_row, via, from_row, to_col, from_col, line,
-    load_sem, send_sem, recv_sem, z_send_sem, z_recv_sem, ready_sem,
+    load_sem, send_sem, recv_sem, z_send_sem, z_recv_sem, ready_sem, round_sem,
 ):
     row, col = lax.axis_index("row"), lax.axis_index("col")
     plane = rows // GROUPS
@@ -89,17 +89,68 @@
     def signal(semaphore, peer):
         pl.semaphore_signal(semaphore, inc=1, device_id=peer, device_id_type=MESH)
 
+    def in_plane(x_step, y_step):
+        x = lax.rem(lax.rem(place, 4) + x_step, 4)
+        y = lax.rem(place // 4 + y_step, 4)
+        return row - place + 4 * y + x, col
+
+    flip = lax.rem(group % 2 + group // 2, 2)
+    step_a, step_b = 1 + 2 * flip, 3 - 2 * flip
+    peer_a = (in_group(step_a) + place, col)
+    peer_b = (in_group(step_b) + place, col)
+    z_lo = col // 2
+    adjacent = [
+        in_plane(1, 0),
+        in_plane(3, 0),
+        in_plane(0, 1),
+        in_plane(0, 3),
+        (row, col + 1 - 2 * lax.rem(col, 2)),
+    ]
+    n_adjacent = len(adjacent) + 1 + z_lo * (3 - z_lo) // 2
+
+    def signal_adjacent(semaphore):
+        for peer in adjacent:
+            signal(semaphore, peer)
+
+        @pl.when(z_lo > 0)
+        def _():
+            signal(semaphore, (row, col - 2))
+
+        @pl.when(z_lo < 3)
+        def _():
+            signal(semaphore, (row, col + 2))
+
     barrier = pltpu.get_barrier_semaphore()
-    for step in (1, GROUPS - 1):
-        signal(barrier, (in_group(step) + place, col))
-
-    @pl.loop(1, plane)
-    def _(i):
-        signal(barrier, (in_group(0) + lax.rem(place + i, plane), col))
-
-    @pl.loop(1, cols)
-    def _(i):
-        signal(barrier, (row, lax.rem(col + i, cols)))
+    n_lower = group % 2 + 2 * (group // 2) * (1 - group % 2)
+
+    @pl.when(group == 0)
+    def _():
+        signal(barrier, peer_a)
+
+    @pl.when(group != 2)
+    def _():
+        signal(barrier, peer_b)
+
+    signal_adjacent(barrier)
+
+    def answer():
+        @pl.when(group == 1)
+        def _():
+            signal(ready_sem.at[0], peer_a)
+
+        @pl.when(group >= 2)
+        def _():
+            signal(ready_sem.at[1], peer_a)
+
+        @pl.when(group == 2)
+        def _():
+            signal(ready_sem.at[1], peer_b)
+
+    def tell(k):
+        signal_adjacent(round_sem.at[k])
+
+    def hear(k):
+        pl.semaphore_wait(round_sem.at[k], n_adjacent)
 
     def table_part(step):
         at = pl.ds(pl.multiple_of(in_group(step) * 8, 128), plane * 8)
@@ -108,8 +159,8 @@
     near = (1, GROUPS - 1)
     sources = [
         (x_hbm.at[0], x.at[0]),
-        table_part(1),
-        table_part(GROUPS - 1),
+        table_part(step_a),
+        table_part(step_b),
         table_part(2),
         table_part(0),
         (x_hbm.at[1], x.at[1]),
@@ -210,24 +261,47 @@
 
     loads[0].wait()
     split(0)
-    for k, step in enumerate((*near, 2, 0)):
-        loads[1 + k].wait()
+    loads[1].wait()
+    first(0, step_a)
+    pl.semaphore_wait(barrier, n_lower + n_adjacent)
+    answer()
+    tell(0)
+
+    @pl.when(group == 0)
+    def _():
+        pl.semaphore_wait(ready_sem.at[0], 1)
+
+    z_copy(0, step_a).start()
+    loads[2].wait()
+    first(0, step_b)
+
+    @pl.when(group != 2)
+    def _():
+        pl.semaphore_wait(ready_sem.at[1], 1)
+
+    z_copy(0, step_b).start()
+    for peer in (peer_a, peer_b):
+        signal(ready_sem.at[2], peer)
+    for k, step in ((3, 2), (4, 0)):
+        loads[k].wait()
         first(0, step)
-        if k == 0:
-            pl.semaphore_wait(barrier, plane + cols)
-            for other in near:
-                signal(ready_sem, (in_group(other) + place, col))
-        if step in near:
-            z_copy(0, step).start()
-    send_plane(0, 0)
-    pl.semaphore_wait(ready_sem, 2)
-    z_copy(0, 2).start()
+    hear(0)
+    tell(1)
     loads[5].wait()
     split(1)
-    for step in (*near, 2, 0):
-        first(1, step)
-        if step:
-            z_copy(1, step).start()
+    first(1, step_a)
+    hear(1)
+    tell(2)
+    pl.semaphore_wait(ready_sem.at[2], 2)
+    z_copy(0, 2).start()
+    z_copy(1, step_a).start()
+    first(1, step_b)
+    z_copy(1, step_b).start()
+    first(1, 2)
+    z_copy(1, 2).start()
+    first(1, 0)
+    hear(2)
+    send_plane(0, 0)
     send_plane(1, 0)
     loads[6].wait()
     for f in range(2):
@@ -306,7 +380,8 @@
             pltpu.SemaphoreType.DMA((6,)),
             pltpu.SemaphoreType.DMA((6,)),
             pltpu.SemaphoreType.DMA((6,)),
-            pltpu.SemaphoreType.REGULAR,
+            pltpu.SemaphoreType.REGULAR((3,)),
+            pltpu.SemaphoreType.REGULAR((3,)),
         ],
         compiler_params=pltpu.CompilerParams(
             collective_id=0, has_side_effects=True, vmem_limit_bytes=VMEM_LIMIT

time: 86.1 us -> 84.2 us (0.978)
  Pallas kernels: 85.9 us -> 84 us
    pallas_call x1, Pallas kernels: 84.8 us -> 82.9 us  [on_device(): pl.pallas_call(functools.partial(kernel, rows, cols), out_shape=result, i...]
where the time goes in v4:
time: 84.2 us; the launch traced here: 84 us
  Pallas kernels  84 us (100%)
    pallas_call x1, Pallas kernels, on_device(): pl.pallas_call(functools.partial(kernel, rows, cols), out_shape=result, i...  82.9 us

profile of v4, /device:TPU:1, one launch (start us, length us, event | category | flops | bytes accessed | tf_op | source)
XLA Modules:
  0.0 84.0 jit_solution(4847116322601367307)
XLA Ops:
  0.0 0.0 copy-start
  0.0 0.0 copy-start.1
  0.0 0.0 copy-start.2
  0.0 82.9 %shard_map.55.spectrum = f32[2,8,64,256]{3,2,1,0:T(8,128)S(1)} custom-call(f32[2,256,512]{2,1,0:T(8,128)} %bitcast.9, bf16[2,768,512]{2,1,0:T(8,128)(2,1)} %constant.2.clone.h_hbm), custom_call_target="tpu_custom_call" | custom-call | tf_op jit(solution)/shard_map/pallas_call | solution.py:361
  82.9 0.0 copy-done
  82.9 0.0 copy-done.1
  82.9 0.0 copy-done.2
  82.9 1.1 %shard_map.56 = f32[2,8,64,256]{3,2,1,0:T(8,128)} custom-call(f32[2,8,64,256]{3,2,1,0:T(8,128)S(1)} %shard_map.55.spectrum, f32[1,512]{1,0:T(1,128)S(1)} %bitcast.6, f32[1,512]{1,0:T(1,128)S(1)} %bitcast.7, f32[1,256]{1,0:T(1,128)S(1)} %bitcast.8), custom_call_target="tpu_custom_call" | custom-call | tf_op jit(solution)/shard_map/pallas_call | solution.py:390
Async XLA Ops:
  0.0 82.9 %copy-start = (f32[512]{0:T(512)S(1)}, f32[512]{0:T(512)}, u32[]{:S(2)}) copy-start(f32[512]{0:T(512)} %param.6) | copy-start | bytes 6148
  0.0 82.9 %copy-start.1 = (f32[512]{0:T(512)S(1)}, f32[512]{0:T(512)}, u32[]{:S(2)}) copy-start(f32[512]{0:T(512)} %param.7) | copy-start | bytes 6148
  0.0 82.9 %copy-start.2 = (f32[256]{0:T(256)S(1)}, f32[256]{0:T(256)}, u32[]{:S(2)}) copy-start(f32[256]{0:T(256)} %param.8) | copy-start | bytes 3076

commit v5 on v4

--- a/solution.py
+++ b/solution.py
@@ -98,27 +98,39 @@
     step_a, step_b = 1 + 2 * flip, 3 - 2 * flip
     peer_a = (in_group(step_a) + place, col)
     peer_b = (in_group(step_b) + place, col)
-    z_lo = col // 2
+    z_lo, core = col // 2, lax.rem(col, 2)
+    x_at, y_at = lax.rem(place, 4), place // 4
     adjacent = [
-        in_plane(1, 0),
-        in_plane(3, 0),
-        in_plane(0, 1),
-        in_plane(0, 3),
-        (row, col + 1 - 2 * lax.rem(col, 2)),
+        (x_at < 3, in_plane(1, 0)),
+        (x_at == 0, in_plane(3, 0)),
+        (y_at < 3, in_plane(0, 1)),
+        (y_at == 0, in_plane(0, 3)),
+        (core == 0, (row, col + 1 - 2 * core)),
     ]
     n_adjacent = len(adjacent) + 1 + z_lo * (3 - z_lo) // 2
-
-    def signal_adjacent(semaphore):
-        for peer in adjacent:
-            signal(semaphore, peer)
-
-        @pl.when(z_lo > 0)
-        def _():
-            signal(semaphore, (row, col - 2))
-
-        @pl.when(z_lo < 3)
-        def _():
-            signal(semaphore, (row, col + 2))
+    n_before = (x_at + 1) // 2 + (y_at + 1) // 2 + core + (z_lo + 3) // 4
+
+    def signal_adjacent(semaphore, later, earlier):
+        for is_later, peer in adjacent:
+            if later and earlier:
+                signal(semaphore, peer)
+            else:
+
+                @pl.when(is_later if later else jnp.logical_not(is_later))
+                def _():
+                    signal(semaphore, peer)
+
+        if earlier:
+
+            @pl.when(z_lo > 0)
+            def _():
+                signal(semaphore, (row, col - 2))
+
+        if later:
+
+            @pl.when(z_lo < 3)
+            def _():
+                signal(semaphore, (row, col + 2))
 
     barrier = pltpu.get_barrier_semaphore()
     n_lower = group % 2 + 2 * (group // 2) * (1 - group % 2)
@@ -131,7 +143,7 @@
     def _():
         signal(barrier, peer_b)
 
-    signal_adjacent(barrier)
+    signal_adjacent(barrier, True, False)
 
     def answer():
         @pl.when(group == 1)
@@ -146,8 +158,10 @@
         def _():
             signal(ready_sem.at[1], peer_b)
 
+        signal_adjacent(round_sem.at[3], False, True)
+
     def tell(k):
-        signal_adjacent(round_sem.at[k])
+        signal_adjacent(round_sem.at[k], True, True)
 
     def hear(k):
         pl.semaphore_wait(round_sem.at[k], n_adjacent)
@@ -178,13 +192,10 @@
         at = pl.ds(top, plane * 8)
         mid[...] = product((h[0, at], h[1, at]), (xs[f, 0], xs[f, 1]), ((1,), (1,)))
 
-        @pl.loop(0, plane // 4)
-        def _(g):
-            for k in range(4):
-                here = pl.ds(pl.multiple_of((g * 4 + k) * 8, 8), 8)
-                v = swap_granules(mid[here, :128], mid[here, 128:])
-                to_row[f, in_group(step) + g * 4 + k, :, :128] = v[0]
-                to_row[f, in_group(step) + g * 4 + k, :, 128:] = v[1]
+        for q in range(plane):
+            v = swap_granules(mid[8 * q : 8 * q + 8, :128], mid[8 * q : 8 * q + 8, 128:])
+            to_row[f, in_group(step) + q, :, :128] = v[0]
+            to_row[f, in_group(step) + q, :, 128:] = v[1]
 
     def split(f):
         xs[f, 0], xs[f, 1] = halves(x[f])
@@ -247,25 +258,31 @@
         )
 
     def third(f, part):
-        @pl.loop(0, 8)
-        def _(g):
-            at = pl.ds(pl.multiple_of(g * 8, 8), 8)
+        for g in range(8):
+            at = slice(8 * g, 8 * g + 8)
             for j in range(2):
                 v = swap_four([from_col[f, part, 4 * j + c, at] for c in range(4)])
                 for k in range(4):
-                    line[k, at, pl.ds(128 * j, 128)] = v[k]
+                    line[k, at, 128 * j : 128 * j + 128] = v[k]
 
         lines = line[...].reshape(256, 256)
         modes = product(halves(lines), (hz[0], hz[1]), ((1,), (0,)))
         out[f, 4 * part : 4 * part + 4] = modes.reshape(4, 64, 256)
+
+    @pl.when(jnp.logical_and(group != 2, n_lower + n_before > 0))
+    def _():
+        pl.semaphore_wait(barrier, n_lower + n_before)
+        answer()
 
     loads[0].wait()
     split(0)
     loads[1].wait()
     first(0, step_a)
-    pl.semaphore_wait(barrier, n_lower + n_adjacent)
-    answer()
-    tell(0)
+
+    @pl.when(group == 2)
+    def _():
+        pl.semaphore_wait(barrier, n_lower + n_before)
+        answer()
 
     @pl.when(group == 0)
     def _():
@@ -282,6 +299,12 @@
     z_copy(0, step_b).start()
     for peer in (peer_a, peer_b):
         signal(ready_sem.at[2], peer)
+
+    @pl.when(n_adjacent > n_before)
+    def _():
+        pl.semaphore_wait(round_sem.at[3], n_adjacent - n_before)
+
+    tell(0)
     for k, step in ((3, 2), (4, 0)):
         loads[k].wait()
         first(0, step)
@@ -381,7 +404,7 @@
             pltpu.SemaphoreType.DMA((6,)),
             pltpu.SemaphoreType.DMA((6,)),
             pltpu.SemaphoreType.REGULAR((3,)),
-            pltpu.SemaphoreType.REGULAR((3,)),
+            pltpu.SemaphoreType.REGULAR((4,)),
         ],
         compiler_params=pltpu.CompilerParams(
             collective_id=0, has_side_effects=True, vmem_limit_bytes=VMEM_LIMIT

time: 84.2 us -> 82.4 us (0.979); the launches traced: 84 us -> 81.1 us
  Pallas kernels: 84 us -> 81 us
    pallas_call x1, Pallas kernels: 82.9 us -> 79.9 us  [on_device(): pl.pallas_call(functools.partial(kernel, rows, cols), out_shape=result, i...]
where the time goes in v5:
time: 82.4 us; the launch traced here: 81.1 us
  Pallas kernels  81 us (98%)
    pallas_call x1, Pallas kernels, on_device(): pl.pallas_call(functools.partial(kernel, rows, cols), out_shape=result, i...  79.9 us

profile of v5, /device:TPU:1, one launch (start us, length us, event | category | flops | bytes accessed | tf_op | source)
XLA Modules:
  0.0 81.1 jit_solution(14806489496484539581)
XLA Ops:
  0.0 0.0 copy-start
  0.0 0.0 copy-start.1
  0.0 0.0 copy-start.2
  0.0 79.9 %shard_map.55.spectrum = f32[2,8,64,256]{3,2,1,0:T(8,128)S(1)} custom-call(f32[2,256,512]{2,1,0:T(8,128)} %bitcast.9, bf16[2,768,512]{2,1,0:T(8,128)(2,1)} %constant.2.clone.h_hbm), custom_call_target="tpu_custom_call" | custom-call | tf_op jit(solution)/shard_map/pallas_call | solution.py:384
  79.9 0.0 copy-done
  79.9 0.0 copy-done.1
  79.9 0.0 copy-done.2
  79.9 1.1 %shard_map.56 = f32[2,8,64,256]{3,2,1,0:T(8,128)} custom-call(f32[2,8,64,256]{3,2,1,0:T(8,128)S(1)} %shard_map.55.spectrum, f32[1,512]{1,0:T(1,128)S(1)} %bitcast.6, f32[1,512]{1,0:T(1,128)S(1)} %bitcast.7, f32[1,256]{1,0:T(1,128)S(1)} %bitcast.8), custom_call_target="tpu_custom_call" | custom-call | tf_op jit(solution)/shard_map/pallas_call | solution.py:413
Async XLA Ops:
  0.0 79.9 %copy-start = (f32[512]{0:T(512)S(1)}, f32[512]{0:T(512)}, u32[]{:S(2)}) copy-start(f32[512]{0:T(512)} %param.6) | copy-start | bytes 6148
  0.0 79.9 %copy-start.1 = (f32[512]{0:T(512)S(1)}, f32[512]{0:T(512)}, u32[]{:S(2)}) copy-start(f32[512]{0:T(512)} %param.7) | copy-start | bytes 6148
  0.0 79.9 %copy-start.2 = (f32[256]{0:T(256)S(1)}, f32[256]{0:T(256)}, u32[]{:S(2)}) copy-start(f32[256]{0:T(256)} %param.8) | copy-start | bytes 3076

commit v6 on v5

--- a/solution.py
+++ b/solution.py
@@ -13,6 +13,7 @@
 F32 = jnp.float32
 BF16 = jnp.bfloat16
 GROUPS = 4
+NB = 4
 VMEM_LIMIT = 53500 * 2**10
 
 
@@ -76,8 +77,9 @@
 
 
 def kernel(
-    rows, cols, x_hbm, h_hbm, out, x, xs, h, hz, mid, to_row, via, from_row, to_col, from_col, line,
-    load_sem, send_sem, recv_sem, z_send_sem, z_recv_sem, ready_sem, round_sem,
+    rows, cols, x_hbm, h_hbm, out, x, xs, h, hz, mid, to_row, via, relay, from_row, to_col, from_col, line,
+    load_sem, send_sem, recv_sem, z_send_sem, z_recv_sem, relay_sem, on_sem,
+    ready_sem, round_sem,
 ):
     row, col = lax.axis_index("row"), lax.axis_index("col")
     plane = rows // GROUPS
@@ -208,6 +210,50 @@
             device_id=(in_group(step) + place, col), device_id_type=MESH,
         )
 
+    def far_copy(f):
+        return pltpu.make_async_remote_copy(
+            to_row.at[f, pl.ds(in_group(2) + NB, plane - NB)], via.at[f, 1, pl.ds(NB, plane - NB)],
+            z_send_sem.at[f * 3 + 1], z_recv_sem.at[f * 3 + 1],
+            device_id=(in_group(2) + place, col), device_id_type=MESH,
+        )
+
+    def relay_copy(f, side):
+        return pltpu.make_async_remote_copy(
+            to_row.at[f, pl.ds(in_group(2), NB)], relay.at[f, side],
+            z_send_sem.at[f * 3 + 1], relay_sem.at[2 * f + side],
+            device_id=peer_b, device_id_type=MESH,
+        )
+
+    def on_copy(f, side):
+        return pltpu.make_async_remote_copy(
+            relay.at[f, side], via.at[f, 1, pl.ds(0, NB)],
+            on_sem.at[2 * f + side], z_recv_sem.at[f * 3 + 1],
+            device_id=peer_a if side else peer_b, device_id_type=MESH,
+        )
+
+    odd = lax.rem(group, 2) == 1
+
+    def start_far(f):
+        @pl.when(odd)
+        def _():
+            far_copy(f).start()
+
+        @pl.when(jnp.logical_not(odd))
+        def _():
+            z_copy(f, 2).start()
+
+    def start_relay(f):
+        @pl.when(odd)
+        def _():
+            relay_copy(f, group // 2).start()
+
+    def send_on(f):
+        @pl.when(group == 2)
+        def _():
+            for side in range(2):
+                relay_copy(f, side).wait_recv()
+                on_copy(f, side).start()
+
     def send_plane(f, step):
         source = in_group(GROUPS - step) + place if step else row
 
@@ -291,11 +337,14 @@
     z_copy(0, step_a).start()
     loads[2].wait()
     first(0, step_b)
+    loads[3].wait()
+    first(0, 2)
 
     @pl.when(group != 2)
     def _():
         pl.semaphore_wait(ready_sem.at[1], 1)
 
+    start_relay(0)
     z_copy(0, step_b).start()
     for peer in (peer_a, peer_b):
         signal(ready_sem.at[2], peer)
@@ -305,9 +354,8 @@
         pl.semaphore_wait(round_sem.at[3], n_adjacent - n_before)
 
     tell(0)
-    for k, step in ((3, 2), (4, 0)):
-        loads[k].wait()
-        first(0, step)
+    loads[4].wait()
+    first(0, 0)
     hear(0)
     tell(1)
     loads[5].wait()
@@ -316,12 +364,14 @@
     hear(1)
     tell(2)
     pl.semaphore_wait(ready_sem.at[2], 2)
-    z_copy(0, 2).start()
+    start_far(0)
+    send_on(0)
     z_copy(1, step_a).start()
     first(1, step_b)
+    first(1, 2)
+    start_relay(1)
     z_copy(1, step_b).start()
-    first(1, 2)
-    z_copy(1, 2).start()
+    start_far(1)
     first(1, 0)
     hear(2)
     send_plane(0, 0)
@@ -331,6 +381,8 @@
         for step in (*near, 2):
             z_copy(f, step).wait_recv()
             send_plane(f, step)
+        if f == 0:
+            send_on(1)
         all_rows(f).wait_recv()
         second(f)
         for part in range(2):
@@ -345,6 +397,11 @@
         all_rows(f).wait_send()
         for part in range(2):
             all_cols(f, part).wait_send()
+
+        @pl.when(group == 2)
+        def _():
+            for side in range(2):
+                on_copy(f, side).wait_send()
 
 
 def divide(spectrum, sx, sy, sz, out, done, sems):
@@ -394,6 +451,7 @@
             pltpu.VMEM((nx // GROUPS, ny * nz), F32),
             pltpu.VMEM((fields, rows, 8, 256), F32),
             pltpu.VMEM((fields, GROUPS - 1, rows // GROUPS, 8, 256), F32),
+            pltpu.VMEM((fields, 2, NB, 8, 256), F32),
             pltpu.VMEM((fields, rows, 8, 256), F32),
             pltpu.VMEM((fields, 2, cols, 64, 128), F32),
             pltpu.VMEM((fields, 2, cols, 64, 128), F32),
@@ -403,6 +461,8 @@
             pltpu.SemaphoreType.DMA((6,)),
             pltpu.SemaphoreType.DMA((6,)),
             pltpu.SemaphoreType.DMA((6,)),
+            pltpu.SemaphoreType.DMA((4,)),
+            pltpu.SemaphoreType.DMA((4,)),
             pltpu.SemaphoreType.REGULAR((3,)),
             pltpu.SemaphoreType.REGULAR((4,)),
         ],

time: 82.4 us -> 81.3 us (0.987)
  the two profiles are of different devices: /device:TPU:1 before, /device:TPU:225 now
where the time goes in v6:
time: 81.3 us; the launch traced here: 81.2 us
  Pallas kernels  81.2 us (100%)
    pallas_call x1, Pallas kernels, on_device(): pl.pallas_call(functools.partial(kernel, rows, cols), out_shape=result, i...  80 us

profile of v6, /device:TPU:225, one launch (start us, length us, event | category | flops | bytes accessed | tf_op | source)
XLA Modules:
  0.0 81.2 jit_solution(3863568736374343387)
XLA Ops:
  0.0 0.0 copy-start
  0.0 0.0 copy-start.1
  0.0 0.0 copy-start.2
  0.0 80.0 %shard_map.55.spectrum = f32[2,8,64,256]{3,2,1,0:T(8,128)S(1)} custom-call(f32[2,256,512]{2,1,0:T(8,128)} %bitcast.9, bf16[2,768,512]{2,1,0:T(8,128)(2,1)} %constant.2.clone.h_hbm), custom_call_target="tpu_custom_call" | custom-call | tf_op jit(solution)/shard_map/pallas_call | solution.py:441
  80.0 0.0 copy-done
  80.1 0.0 copy-done.1
  80.1 0.0 copy-done.2
  80.1 1.1 %shard_map.56 = f32[2,8,64,256]{3,2,1,0:T(8,128)} custom-call(f32[2,8,64,256]{3,2,1,0:T(8,128)S(1)} %shard_map.55.spectrum, f32[1,512]{1,0:T(1,128)S(1)} %bitcast.6, f32[1,512]{1,0:T(1,128)S(1)} %bitcast.7, f32[1,256]{1,0:T(1,128)S(1)} %bitcast.8), custom_call_target="tpu_custom_call" | custom-call | tf_op jit(solution)/shard_map/pallas_call | solution.py:473
Async XLA Ops:
  0.0 80.0 %copy-start = (f32[512]{0:T(512)S(1)}, f32[512]{0:T(512)}, u32[]{:S(2)}) copy-start(f32[512]{0:T(512)} %param.6) | copy-start | bytes 6148
  0.0 80.1 %copy-start.1 = (f32[512]{0:T(512)S(1)}, f32[512]{0:T(512)}, u32[]{:S(2)}) copy-start(f32[512]{0:T(512)} %param.7) | copy-start | bytes 6148
  0.0 80.1 %copy-start.2 = (f32[256]{0:T(256)S(1)}, f32[256]{0:T(256)}, u32[]{:S(2)}) copy-start(f32[256]{0:T(256)} %param.8) | copy-start | bytes 3076

commit v7 on v6

--- a/solution.py
+++ b/solution.py
@@ -186,7 +186,7 @@
         pltpu.make_async_copy(src, dst, load_sem.at[k])
         for k, (src, dst) in enumerate(sources)
     ]
-    for load in loads:
+    for load in loads[:2]:
         load.start()
 
     def first(f, step):
@@ -321,6 +321,8 @@
         answer()
 
     loads[0].wait()
+    for load in loads[2:]:
+        load.start()
     split(0)
     loads[1].wait()
     first(0, step_a)

time: 81.3 us -> 81.3 us (level)
  the two profiles are of different devices: /device:TPU:225 before, /device:TPU:129 now
where the time goes in v7:
time: 81.3 us; the launch traced here: 81.2 us
  Pallas kernels  81.1 us (100%)
    pallas_call x1, Pallas kernels, on_device(): pl.pallas_call(functools.partial(kernel, rows, cols), out_shape=result, i...  80 us

profile of v7, /device:TPU:129, one launch (start us, length us, event | category | flops | bytes accessed | tf_op | source)
XLA Modules:
  0.0 81.2 jit_solution(17870048885518046488)
XLA Ops:
  0.0 0.0 copy-start
  0.0 0.0 copy-start.1
  0.0 0.0 copy-start.2
  0.0 80.0 %shard_map.55.spectrum = f32[2,8,64,256]{3,2,1,0:T(8,128)S(1)} custom-call(f32[2,256,512]{2,1,0:T(8,128)} %bitcast.9, bf16[2,768,512]{2,1,0:T(8,128)(2,1)} %constant.2.clone.h_hbm), custom_call_target="tpu_custom_call" | custom-call | tf_op jit(solution)/shard_map/pallas_call | solution.py:443
  80.0 0.0 copy-done
  80.0 0.0 copy-done.1
  80.1 0.0 copy-done.2
  80.1 1.1 %shard_map.56 = f32[2,8,64,256]{3,2,1,0:T(8,128)} custom-call(f32[2,8,64,256]{3,2,1,0:T(8,128)S(1)} %shard_map.55.spectrum, f32[1,512]{1,0:T(1,128)S(1)} %bitcast.6, f32[1,512]{1,0:T(1,128)S(1)} %bitcast.7, f32[1,256]{1,0:T(1,128)S(1)} %bitcast.8), custom_call_target="tpu_custom_call" | custom-call | tf_op jit(solution)/shard_map/pallas_call | solution.py:475
Async XLA Ops:
  0.0 80.0 %copy-start = (f32[512]{0:T(512)S(1)}, f32[512]{0:T(512)}, u32[]{:S(2)}) copy-start(f32[512]{0:T(512)} %param.6) | copy-start | bytes 6148
  0.0 80.0 %copy-start.1 = (f32[512]{0:T(512)S(1)}, f32[512]{0:T(512)}, u32[]{:S(2)}) copy-start(f32[512]{0:T(512)} %param.7) | copy-start | bytes 6148
  0.0 80.0 %copy-start.2 = (f32[256]{0:T(256)S(1)}, f32[256]{0:T(256)}, u32[]{:S(2)}) copy-start(f32[256]{0:T(256)} %param.8) | copy-start | bytes 3076

commit v8 on v7

--- a/solution.py
+++ b/solution.py
@@ -421,12 +421,8 @@
         symbol = (part_x + part_y) + sz[...]
         for f in range(fields):
             done[f, k] = spectrum[f, k] / symbol
-        if k % 2 == 1:
-            two = pl.ds(k - 1, 2)
-            copies.append(
-                pltpu.make_async_copy(done.at[:, two], out.at[:, two], sems.at[k // 2])
-            )
-            copies[-1].start()
+        copies.append(pltpu.make_async_copy(done.at[:, k], out.at[:, k], sems.at[k]))
+        copies[-1].start()
     for copy in copies:
         copy.wait()
 
@@ -479,7 +475,7 @@
         out_specs=in_hbm,
         scratch_shapes=[
             pltpu.VMEM(result.shape, F32),
-            pltpu.SemaphoreType.DMA((share_x // 2,)),
+            pltpu.SemaphoreType.DMA((share_x,)),
         ],
         compiler_params=pltpu.CompilerParams(vmem_limit_bytes=8 * 2**20),
     )(spectrum, symbol_x[None], symbol_y[None], symbol_z[None])

time: 81.3 us -> 81.4 us (level)
  no operation moved by 1% of the time
where the time goes in v8:
time: 81.4 us; the launch traced here: 81.2 us
  Pallas kernels  81.2 us (100%)
    pallas_call x1, Pallas kernels, on_device(): pl.pallas_call(functools.partial(kernel, rows, cols), out_shape=result, i...  80 us

profile of v8, /device:TPU:129, one launch (start us, length us, event | category | flops | bytes accessed | tf_op | source)
XLA Modules:
  0.0 81.2 jit_solution(10874211779327820186)
XLA Ops:
  0.0 0.0 copy-start
  0.0 0.0 copy-start.1
  0.0 0.0 copy-start.2
  0.0 80.0 %shard_map.55.spectrum = f32[2,8,64,256]{3,2,1,0:T(8,128)S(1)} custom-call(f32[2,256,512]{2,1,0:T(8,128)} %bitcast.9, bf16[2,768,512]{2,1,0:T(8,128)(2,1)} %constant.2.clone.h_hbm), custom_call_target="tpu_custom_call" | custom-call | tf_op jit(solution)/shard_map/pallas_call | solution.py:439
  80.0 0.0 copy-done
  80.0 0.0 copy-done.1
  80.1 0.0 copy-done.2
  80.1 1.2 %shard_map.56 = f32[2,8,64,256]{3,2,1,0:T(8,128)} custom-call(f32[2,8,64,256]{3,2,1,0:T(8,128)S(1)} %shard_map.55.spectrum, f32[1,512]{1,0:T(1,128)S(1)} %bitcast.6, f32[1,512]{1,0:T(1,128)S(1)} %bitcast.7, f32[1,256]{1,0:T(1,128)S(1)} %bitcast.8), custom_call_target="tpu_custom_call" | custom-call | tf_op jit(solution)/shard_map/pallas_call | solution.py:471
Async XLA Ops:
  0.0 80.0 %copy-start = (f32[512]{0:T(512)S(1)}, f32[512]{0:T(512)}, u32[]{:S(2)}) copy-start(f32[512]{0:T(512)} %param.6) | copy-start | bytes 6148
  0.0 80.0 %copy-start.1 = (f32[512]{0:T(512)S(1)}, f32[512]{0:T(512)}, u32[]{:S(2)}) copy-start(f32[512]{0:T(512)} %param.7) | copy-start | bytes 6148
  0.0 80.0 %copy-start.2 = (f32[256]{0:T(256)S(1)}, f32[256]{0:T(256)}, u32[]{:S(2)}) copy-start(f32[256]{0:T(256)} %param.8) | copy-start | bytes 3076
